TPU v7x, 32 devices: a whole 2x2x4 slice. The times are simulated.
32 devices in a mesh: seq: 2 (over y), dp: 16 (over z, x, core).
Axes of the slice: x: 2, y: 2, z: 4, core: 2. Of those that a mesh axis runs over, the one named last changes fastest.
Arguments:
- inputs: bfloat16 [16, 2, 1024, 768], P('dp', None, 'seq'), may hold values from -6 to 6
- query_weight: bfloat16 [768, 768], P(('seq', 'dp')), may hold values from -0.21875 to 0.21875
- key_weight: bfloat16 [768, 768], P(('seq', 'dp')), may hold values from -0.21875 to 0.21875
- value_weight: bfloat16 [768, 768], P(('seq', 'dp')), may hold values from -0.21875 to 0.21875
- query_bias: bfloat16 [768], P(('seq', 'dp')), may hold values from -3 to 3
- value_bias: bfloat16 [768], P(('seq', 'dp')), may hold values from -3 to 3
- output_weight: bfloat16 [768, 768], P(('seq', 'dp')), may hold values from -2.5 to 2.5
- output_bias: bfloat16 [768], P(('seq', 'dp')), may hold values from -3 to 3
- first_gain: bfloat16 [768], P(('seq', 'dp')), may hold values from 0.099609375 to 1.8984375
- first_shift: bfloat16 [768], P(('seq', 'dp')), may hold values from -3 to 3
- inner_weight: bfloat16 [768, 3072], P(('seq', 'dp')), may hold values from -0.21875 to 0.21875
- inner_bias: bfloat16 [3072], P(('seq', 'dp')), may hold values from -3 to 3
- outer_weight: bfloat16 [3072, 768], P(('seq', 'dp')), may hold values from -0.109375 to 0.109375
- outer_bias: bfloat16 [768], P(('seq', 'dp')), may hold values from -3 to 3
- second_gain: bfloat16 [768], P(('seq', 'dp')), may hold values from 0.099609375 to 1.8984375
- second_shift: bfloat16 [768], P(('seq', 'dp')), may hold values from -3 to 3
- prefix: int32 [16, 2], P('dp'), may hold values from 102 to 512, as said below
- cotangent: bfloat16 [16, 2, 1024, 768], P('dp', None, 'seq'), may hold values from -6 to 6
Outputs:
- outputs: bfloat16 [16, 2, 1024, 768], P('dp', None, 'seq')
- input_grad: float32 [16, 2, 1024, 768], P('dp', None, 'seq')
- grad_query_weight: float32 [768, 768], P(('seq', 'dp'))
- grad_key_weight: float32 [768, 768], P(('seq', 'dp'))
- grad_value_weight: float32 [768, 768], P(('seq', 'dp'))
- grad_query_bias: float32 [768], P(('seq', 'dp'))
- grad_value_bias: float32 [768], P(('seq', 'dp'))
- grad_output_weight: float32 [768, 768], P(('seq', 'dp'))
- grad_output_bias: float32 [768], P(('seq', 'dp'))
- grad_first_gain: float32 [768], P(('seq', 'dp'))
- grad_first_shift: float32 [768], P(('seq', 'dp'))
- grad_inner_weight: float32 [768, 3072], P(('seq', 'dp'))
- grad_inner_bias: float32 [3072], P(('seq', 'dp'))
- grad_outer_weight: float32 [3072, 768], P(('seq', 'dp'))
- grad_outer_bias: float32 [768], P(('seq', 'dp'))
- grad_second_gain: float32 [768], P(('seq', 'dp'))
- grad_second_shift: float32 [768], P(('seq', 'dp'))
Inputs may be any that keep to these rules, and one draw needn't show every extreme that they name: `prefix`: the number of leading tokens of each sequence that attend to one another both ways; some sequence has 512 and some 1024 // 10.
All inputs are finite; a program needn't handle non-finite values.
Results may differ from a plain program's by a relative error of at most 0.017.
Values may be sent and summed in bfloat16 or wider, within the bound.
A program may use at most 384 MiB of HBM per device.

v0:
```python
import jax
import jax.numpy as jnp
from jax import lax
from jax.sharding import PartitionSpec as P

HEADS = 12
HEAD_DIM = 64
EPS = 1e-05
FAR = 1 << 20
BOTH = ("seq", "dp")
F32 = jnp.float32
BF16 = jnp.bfloat16


def dot(a, b):
    return jnp.dot(a, b, preferred_element_type=F32)


def dot_t(a, b):
    return lax.dot_general(a, b, (((1,), (1,)), ((), ())), preferred_element_type=F32)


def t_dot(a, b):
    return lax.dot_general(a, b, (((0,), (0,)), ((), ())), preferred_element_type=F32)


def norm_parts(v):
    center = v - jnp.mean(v, axis=-1, keepdims=True)
    inv = lax.rsqrt(jnp.mean(center * center, axis=-1, keepdims=True) + EPS)
    return (center * inv, inv)


def norm_grad(grad, unit, inv, gain):
    g = grad * gain
    mean_g = jnp.mean(g, axis=-1, keepdims=True)
    mean_gu = jnp.mean(g * unit, axis=-1, keepdims=True)
    return inv * (g - mean_g - unit * mean_gu)


def heads_of(v):
    return v.reshape(v.shape[0], HEADS, HEAD_DIM)


def attend(q, k, v, key_pos, limit):
    scores = (
        jnp.einsum("qhd,khd->hqk", heads_of(q), heads_of(k), preferred_element_type=F32) * 0.125
    )
    scores = jnp.where((key_pos[None, :] <= limit[:, None])[None], scores, -1e30)
    top = jnp.max(scores, axis=-1, keepdims=True)
    lse = top[..., 0] + jnp.log(jnp.sum(jnp.exp(scores - top), axis=-1))
    probs = jnp.exp(scores - lse[..., None])
    low = probs.astype(BF16)
    mixed = jnp.einsum("hqk,khd->qhd", low, heads_of(v), preferred_element_type=F32)
    return (mixed.reshape(q.shape).astype(BF16), (probs, low))


def attend_back(saved, q, k, v, mixed, grad):
    probs, low = saved
    grad_h = heads_of(grad)
    grad_probs = jnp.einsum("qhd,khd->hqk", grad_h, heads_of(v), preferred_element_type=F32)
    row_dot = jnp.sum(grad_probs * probs, axis=-1, keepdims=True)
    grad_scores = (probs * (grad_probs - row_dot)).astype(BF16)
    gq = jnp.einsum("hqk,khd->qhd", grad_scores, heads_of(k), preferred_element_type=F32) * 0.125
    gk = jnp.einsum("hqk,qhd->khd", grad_scores, heads_of(q), preferred_element_type=F32) * 0.125
    gv = jnp.einsum("hqk,qhd->khd", low, grad_h, preferred_element_type=F32)
    return (
        gq.reshape(q.shape).astype(BF16),
        gk.reshape(k.shape).astype(BF16),
        gv.reshape(v.shape).astype(BF16),
    )


def on_device(
    inputs,
    query_weight,
    key_weight,
    value_weight,
    query_bias,
    value_bias,
    output_weight,
    output_bias,
    first_gain,
    first_shift,
    inner_weight,
    inner_bias,
    outer_weight,
    outer_bias,
    second_gain,
    second_shift,
    prefix,
    cotangent,
):
    micros, rows, width = inputs.shape[1:]
    own = query_weight.shape[0]
    hidden_width = inner_weight.shape[1]
    per = hidden_width // width
    seqs = lax.axis_size("seq")
    seq_at = lax.axis_index("seq")
    first_pos = seq_at * rows
    x = inputs[0]
    flat_x = x.reshape(micros * rows, width)
    row_pos = first_pos + jnp.arange(rows, dtype=jnp.int32)
    if seqs == 2:
        before = lax.ppermute(x, "seq", [(0, 1)])
        key_x = jnp.concatenate([x, before], axis=1)
        key_pos = jnp.concatenate(
            [row_pos, jnp.where(seq_at == 1, jnp.arange(rows, dtype=jnp.int32), FAR)]
        )
    else:
        key_x = lax.all_gather(x, "seq", axis=1, tiled=True)
        key_pos = jnp.arange(seqs * rows, dtype=jnp.int32)
    total_rows = key_x.shape[1]
    flat_key_x = key_x.reshape(micros * total_rows, width)
    vectors = (
        query_bias,
        value_bias,
        output_bias,
        first_gain,
        first_shift,
        outer_bias,
        second_gain,
        second_shift,
    )
    small = jnp.concatenate([jnp.stack(vectors, axis=1), inner_bias.reshape(own, per)], axis=1)
    small_count = small.shape[1]
    small = jnp.pad(small, ((0, 0), (0, 128 - small_count)))
    first_pack = lax.all_gather(
        jnp.concatenate([query_weight, key_weight, value_weight, small], axis=1),
        BOTH,
        axis=0,
        tiled=True,
    )
    second_pack = lax.all_gather(
        jnp.concatenate([output_weight, inner_weight], axis=1), BOTH, axis=0, tiled=True
    )
    full_outer = lax.all_gather(outer_weight, BOTH, axis=0, tiled=True)
    full_query = first_pack[:, :width]
    full_kv = first_pack[:, width : 3 * width]
    small_all = first_pack[:, 3 * width : 3 * width + small_count].astype(F32)
    qb, vb, ob, fg, fs, ub, sg, ss = [small_all[:, i] for i in range(8)]
    ib = small_all[:, 8:].reshape(hidden_width)
    full_output = second_pack[:, :width]
    full_inner = second_pack[:, width:]
    queries = (dot(flat_x, full_query) + qb).astype(BF16).reshape(micros, rows, width)
    kv_bias = jnp.concatenate([jnp.zeros_like(vb), vb])
    keys_values = (
        (dot(flat_key_x, full_kv) + kv_bias).astype(BF16).reshape(micros, total_rows, 2 * width)
    )
    keys, values = (keys_values[..., :width], keys_values[..., width:])
    mixed_parts, saved = ([], [])
    for m in range(micros):
        limit = jnp.maximum(row_pos, prefix[0, m] - 1)
        mixed_m, saved_m = attend(queries[m], keys[m], values[m], key_pos, limit)
        mixed_parts.append(mixed_m)
        saved.append(saved_m)
    mixed = jnp.concatenate(mixed_parts, axis=0)
    unit1, inv1 = norm_parts(flat_x.astype(F32) + dot(mixed, full_output) + ob)
    middle = unit1 * fg + fs
    middle_low = middle.astype(BF16)
    inner = dot(middle_low, full_inner) + ib
    half_cdf = 0.5 * (1.0 + lax.erf(inner * 0.5**0.5))
    hidden = (inner * half_cdf).astype(BF16)
    slope = half_cdf + inner * jnp.exp(-0.5 * inner * inner) * 0.3989422804014327
    unit2, inv2 = norm_parts(middle + dot(hidden, full_outer) + ub)
    result = (unit2 * sg + ss).astype(BF16)
    cot = cotangent[0].reshape(micros * rows, width).astype(F32)
    g_sgain = jnp.sum(cot * unit2, axis=0)
    g_sshift = jnp.sum(cot, axis=0)
    grad_mid2 = norm_grad(cot, unit2, inv2, sg)
    grad_outer = grad_mid2.astype(BF16)
    g_ubias = jnp.sum(grad_outer.astype(F32), axis=0)
    g_outer = t_dot(hidden, grad_outer).astype(BF16)
    own_outer = lax.psum_scatter(g_outer, BOTH, scatter_dimension=0, tiled=True).astype(F32)
    grad_hidden = dot_t(grad_outer, full_outer).astype(BF16)
    grad_inner = (grad_hidden.astype(F32) * slope).astype(BF16)
    g_ibias = jnp.sum(grad_inner.astype(F32), axis=0)
    g_inner = t_dot(middle_low, grad_inner)
    grad_middle = grad_mid2 + dot_t(grad_inner, full_inner)
    g_fgain = jnp.sum(grad_middle * unit1, axis=0)
    g_fshift = jnp.sum(grad_middle, axis=0)
    grad_sum1 = norm_grad(grad_middle, unit1, inv1, fg)
    grad_branch = grad_sum1.astype(BF16)
    g_obias = jnp.sum(grad_branch.astype(F32), axis=0)
    g_output = t_dot(mixed, grad_branch)
    own_second = lax.psum_scatter(
        jnp.concatenate([g_output, g_inner], axis=1).astype(BF16),
        BOTH,
        scatter_dimension=0,
        tiled=True,
    ).astype(F32)
    grad_mixed = dot_t(grad_branch, full_output).astype(BF16).reshape(micros, rows, width)
    gq_parts, gk_parts, gv_parts = ([], [], [])
    for m in range(micros):
        gq, gk, gv = attend_back(
            saved[m], queries[m], keys[m], values[m], mixed_parts[m], grad_mixed[m]
        )
        gq_parts.append(gq)
        gk_parts.append(gk)
        gv_parts.append(gv)
    grad_q = jnp.concatenate(gq_parts, axis=0)
    grad_kv = jnp.concatenate([jnp.stack(gk_parts), jnp.stack(gv_parts)], axis=-1)
    flat_kv = grad_kv.reshape(micros * total_rows, 2 * width)
    g_qbias = jnp.sum(grad_q.astype(F32), axis=0)
    g_vbias = jnp.sum(flat_kv[:, width:].astype(F32), axis=0)
    g_query = t_dot(flat_x, grad_q)
    g_kv = t_dot(flat_key_x, flat_kv)
    g_small = jnp.concatenate(
        [
            jnp.stack(
                [g_qbias, g_vbias, g_obias, g_fgain, g_fshift, g_ubias, g_sgain, g_sshift], axis=1
            ),
            g_ibias.reshape(width, per),
        ],
        axis=1,
    )
    g_small = jnp.pad(g_small, ((0, 0), (0, 128 - small_count)))
    own_first = lax.psum_scatter(
        jnp.concatenate([g_query, g_kv, g_small], axis=1).astype(BF16),
        BOTH,
        scatter_dimension=0,
        tiled=True,
    ).astype(F32)
    via_kv = dot_t(flat_kv, full_kv).reshape(micros, total_rows, width)
    grad_x = (grad_sum1 + dot_t(grad_q, full_query)).reshape(micros, rows, width)
    if seqs == 2:
        grad_x = grad_x + via_kv[:, :rows]
        grad_x = grad_x + lax.ppermute(via_kv[:, rows:].astype(BF16), "seq", [(1, 0)]).astype(F32)
    else:
        grad_x = grad_x + lax.psum_scatter(via_kv, "seq", scatter_dimension=1, tiled=True)
    vec = own_first[:, 3 * width : 3 * width + small_count]
    v_of = [vec[:, i] for i in range(8)]
    outputs = result.reshape(micros, rows, width)[None]
    return (
        outputs,
        grad_x[None],
        own_first[:, :width],
        own_first[:, width : 2 * width],
        own_first[:, 2 * width : 3 * width],
        v_of[0],
        v_of[1],
        own_second[:, :width],
        v_of[2],
        v_of[3],
        v_of[4],
        own_second[:, width:],
        vec[:, 8:].reshape(own * per),
        own_outer,
        v_of[5],
        v_of[6],
        v_of[7],
    )


def solution(mesh):
    act = P("dp", None, "seq", None)
    mat = P(BOTH, None)
    vec = P(BOTH)
    params = (mat, mat, mat, vec, vec, mat, vec, vec, vec, mat, vec, mat, vec, vec, vec)
    return jax.shard_map(
        on_device,
        mesh=mesh,
        in_specs=(act,) + params + (P("dp", None), act),
        out_specs=(act, act) + params,
        check_vma=False,
    )
```

profile of v0, /device:TPU:0, one launch (start us, length us, event | category | flops | bytes accessed | tf_op | source)
XLA Modules:
  0.0 761.0 jit_solution(18443517237392561761)
XLA Ops:
  30.0 30.2 %collective-permute-done = bf16[2,512,768]{1,2,0:T(8,128)(2,1)} collective-permute-done((bf16[2,512,768]{1,2,0:T(8,128)(2,1)S(1)}, bf16[2,512,768]{1,2,0:T(8,128)(2,1)}, u32[]{:S(2)}, u32[]{:S(2)}) %collective-permute-start) | collective-permute-done | bytes 1572896 | tf_op jit(solution)/shard_map/ppermute | solution.py:104
  68.5 11.6 %all-gather.4.cloned.1.call-done = bf16[768,2432]{1,0:T(8,128)(2,1)} async-done(((bf16[24,2432]{1,0:T(8,128)(2,1)}), bf16[768,2432]{1,0:T(8,128)(2,1)}) %all-gather.4.cloned.1.call-update) | async-done | bytes 3735568 | tf_op jit(solution)/shard_map/all_gather | solution.py:127
  97.6 12.8 %fusion.1 = (f32[12,512]{1,0:T(8,128)S(1)}, f32[12,512,1024]{2,1,0:T(8,128)}) fusion(pred[512,1024]{1,0:T(8,128)(4,1)} %get-tuple-element.56, bf16[512,12,64]{0,2,1:T(8,128)(2,1)} %bitcast.115, bf16[1024,12,64]{0,2,1:T(8,128)(2,1)S(1)} %bitcast.111), kind=kOutput, calls=%fused_computation.11 | convolution fusion | flops 824174592 | bytes 28073984 | tf_op jit(solution)/shard_map/qhd,khd->hqk/dot_general | solution.py:46
  110.4 12.5 %exponential_reduce_fusion = f32[12,512]{1,0:T(8,128)} fusion(f32[12,512,1024]{2,1,0:T(8,128)} %get-tuple-element.60, f32[12,512]{1,0:T(8,128)S(1)} %get-tuple-element.59, pred[512,1024]{1,0:T(8,128)(4,1)S(1)} %copy-done.3), kind=kLoop, calls=%fused_computation.5 | loop fusion | flops 25159680 | bytes 25739264 | tf_op jit(solution)/shard_map/reduce_sum | solution.py:50
  130.8 12.4 %fusion = (f32[12,512]{1,0:T(8,128)S(1)}, f32[12,512,1024]{2,1,0:T(8,128)}) fusion(pred[512,1024]{1,0:T(8,128)(4,1)} %get-tuple-element.55, bf16[512,12,64]{0,2,1:T(8,128)(2,1)} %bitcast.117, bf16[1024,12,64]{0,2,1:T(8,128)(2,1)S(1)} %bitcast.113), kind=kOutput, calls=%fused_computation.10 | convolution fusion | flops 824174592 | bytes 28073984 | tf_op jit(solution)/shard_map/qhd,khd->hqk/dot_general | solution.py:46
  143.2 12.2 %exponential_reduce_fusion.1 = f32[12,512]{1,0:T(8,128)S(1)} fusion(f32[12,512,1024]{2,1,0:T(8,128)} %get-tuple-element.62, f32[12,512]{1,0:T(8,128)S(1)} %get-tuple-element.61, pred[512,1024]{1,0:T(8,128)(4,1)S(1)} %copy-done.7), kind=kLoop, calls=%fused_computation.8 | loop fusion | flops 25159680 | bytes 25739264 | tf_op jit(solution)/shard_map/reduce_sum | solution.py:50
  155.4 12.2 %convolution_convert_fusion.7 = bf16[12,64,512]{2,1,0:T(8,128)(2,1)} fusion(bf16[1024,12,64]{0,2,1:T(8,128)(2,1)S(1)} %bitcast.121, f32[12,512,1024]{2,1,0:T(8,128)} %get-tuple-element.60, f32[12,512]{1,0:T(8,128)S(1)} %log_add_fusion, pred[512,1024]{1,0:T(8,128)(4,1)S(1)} %copy-done.4), kind=kOutput, calls=%fused_computation.85 | convolution fusion | flops 830865408 | bytes 28073984 | tf_op jit(solution)/shard_map/hqk,khd->qhd/dot_general | solution.py:53
  167.6 11.9 %convolution_convert_fusion.8 = bf16[12,64,512]{2,1,0:T(8,128)(2,1)} fusion(bf16[1024,12,64]{0,2,1:T(8,128)(2,1)S(1)} %bitcast.123, f32[12,512,1024]{2,1,0:T(8,128)} %get-tuple-element.62, f32[12,512]{1,0:T(8,128)S(1)} %log_add_fusion.1, pred[512,1024]{1,0:T(8,128)(4,1)S(1)} %copy-done.7), kind=kOutput, calls=%fused_computation.86 | convolution fusion | flops 830865408 | bytes 28073984 | tf_op jit(solution)/shard_map/hqk,khd->qhd/dot_general | solution.py:53
  185.4 10.1 %multiply_convert_fusion.2 = (bf16[1024,3072]{1,0:T(8,128)(2,1)}, f32[1024,3072]{1,0:T(8,128)}) fusion(f32[3072]{0:T(1024)S(1)} %add.172, bf16[768,3840]{1,0:T(8,128)(2,1)S(1)} %bitcast.155, f32[1024,768]{1,0:T(8,128)S(1)} %get-tuple-element.64, f32[768]{0:T(1024)S(1)} %copy-done.50, f32[768]{0:T(1024)S(1)} %get-tuple-element.27, ...), kind=kOutput, calls=%fused_computation.21 | convolution fusion | flops 4854644736 | bytes 26767360 | tf_op jit(solution)/shard_map/dot_general | solution.py:16
  195.5 19.7 %all-gather.8.cloned.1.call-done = bf16[3072,768]{1,0:T(8,128)(2,1)} async-done(((bf16[96,768]{1,0:T(8,128)(2,1)}), bf16[3072,768]{1,0:T(8,128)(2,1)}) %all-gather.8.cloned.1.call-update) | async-done | bytes 4718608 | tf_op jit(solution)/shard_map/all_gather | solution.py:136
  215.2 9.3 %fusion.72 = (f32[1024]{0:T(1024)S(1)}, f32[1024,768]{1,0:T(8,128)S(1)}) fusion(f32[768]{0:T(1024)S(1)} %copy-done.52, bf16[1024,3072]{1,0:T(8,128)(2,1)} %get-tuple-element.65, bf16[3072,768]{1,0:T(8,128)(2,1)} %all-gather.8.cloned.1.call-done, f32[768]{0:T(1024)S(1)} %copy-done.50, f32[768]{0:T(1024)S(1)} %get-tuple-element.27, ...), kind=kOutput, calls=%fused_computation.155 | convolution fusion | flops 4837342208 | bytes 17323008 | tf_op jit(solution)/shard_map/dot_general | solution.py:16
  230.3 14.9 %fusion.73 = (bf16[3072]{0:T(1024)(128)(2,1)}, bf16[1024,3072]{1,0:T(8,128)(2,1)}) fusion(f32[1024,3072]{1,0:T(8,128)} %get-tuple-element.66, f32[3072]{0:T(1024)S(1)} %add.172, bf16[3072,768]{1,0:T(8,128)(2,1)S(1)} %bitcast.159, f32[1024,768]{1,0:T(8,128)S(1)} %get-tuple-element.40), kind=kOutput, calls=%fused_computation.156 | convolution fusion | flops 4876661760 | bytes 26757120 | tf_op jit(solution)/shard_map/dot_general | solution.py:20
  245.2 8.8 %multiply_reduce_fusion.2 = (bf16[768]{0:T(1024)(128)(2,1)}, f32[1024]{0:T(1024)S(1)}, f32[1024]{0:T(1024)S(1)}, bf16[768]{0:T(1024)(128)(2,1)}, f32[1024,768]{1,0:T(8,128)S(1)}) fusion(f32[1024,768]{1,0:T(8,128)S(1)} %copy-done.10, f32[1024]{0:T(1024)S(1)} %add_rsqrt_fusion.1, f32[1024]{0:T(1024)S(1)} %broadcast_multiply_fusion.4, ...), kind=kOutput, calls=%fused_computation.52 | convolution fusion | flops 4839698432 | bytes 20470784 | tf_op jit(solution)/shard_map/dot_general | solution.py:20
  258.6 12.7 %convolution_convert_fusion.3 = bf16[12,64,1024]{2,1,0:T(8,128)(2,1)} fusion(bf16[512,12,64]{0,2,1:T(8,128)(2,1)S(1)} %bitcast.133, f32[12,512,1024]{2,1,0:T(8,128)} %get-tuple-element.62, f32[12,512]{1,0:T(8,128)S(1)} %copy-done.40, pred[512,1024]{1,0:T(8,128)(4,1)S(1)} %copy-done.8), kind=kOutput, calls=%fused_computation.75 | convolution fusion | flops 831258624 | bytes 28073984 | tf_op jit(solution)/shard_map/hqk,qhd->khd/dot_general | solution.py:65
  271.4 21.9 %multiply_reduce_fusion.1 = (f32[12,512]{1,0:T(8,128)}, f32[12,512,1024]{2,1,0:T(8,128)}) fusion(f32[12,512,1024]{2,1,0:T(8,128)} %get-tuple-element.62, f32[12,512]{1,0:T(8,128)S(1)} %copy-done.40, pred[512,1024]{1,0:T(8,128)(4,1)S(1)} %copy-done.8, bf16[512,12,64]{0,2,1:T(8,128)(2,1)S(1)} %bitcast.134, bf16[1024,12,64]{0,2,1:T(8,128)(2,1)S(1)} %bitcast.124), kind=kOutput, calls=%fused_computation.3 | convolution fusion | flops 836757504 | bytes 53264384 | tf_op jit(solution)/shard_map/qhd,khd->hqk/dot_general | solution.py:60
  293.3 17.5 %multiply_convert_fusion.1 = bf16[12,512,1024]{2,1,0:T(8,128)(2,1)S(1)} fusion(f32[12,512,1024]{2,1,0:T(8,128)} %get-tuple-element.73, f32[12,512,1024]{2,1,0:T(8,128)} %get-tuple-element.62, f32[12,512]{1,0:T(8,128)} %get-tuple-element.72, f32[12,512]{1,0:T(8,128)} %copy-done.39, pred[512,1024]{1,0:T(8,128)(4,1)} %get-tuple-element.55), kind=kLoop, calls=%fused_computation.2 | loop fusion | flops 37748736 | bytes 63488000 | tf_op jit(solution)/shard_map/convert_element_type | solution.py:62
  321.8 12.8 %convolution_convert_fusion.2 = bf16[12,64,1024]{2,1,0:T(8,128)(2,1)} fusion(bf16[512,12,64]{0,2,1:T(8,128)(2,1)S(1)} %bitcast.131, f32[12,512,1024]{2,1,0:T(8,128)} %get-tuple-element.60, f32[12,512]{1,0:T(8,128)S(1)} %copy-done.38, pred[512,1024]{1,0:T(8,128)(4,1)S(1)} %copy-done.5), kind=kOutput, calls=%fused_computation.74 | convolution fusion | flops 831258624 | bytes 28073984 | tf_op jit(solution)/shard_map/hqk,qhd->khd/dot_general | solution.py:65
  334.6 21.3 %multiply_reduce_fusion = (f32[12,512]{1,0:T(8,128)S(1)}, f32[12,512,1024]{2,1,0:T(8,128)}) fusion(f32[12,512,1024]{2,1,0:T(8,128)} %get-tuple-element.60, f32[12,512]{1,0:T(8,128)S(1)} %copy-done.38, pred[512,1024]{1,0:T(8,128)(4,1)S(1)} %copy-done.6, bf16[512,12,64]{0,2,1:T(8,128)(2,1)S(1)} %bitcast.132, bf16[1024,12,64]{0,2,1:T(8,128)(2,1)S(1)} %bitcast.122), kind=kOutput, calls=%fused_computation.1 | convolution fusion | flops 836757504 | bytes 53264384 | tf_op jit(solution)/shard_map/qhd,khd->hqk/dot_general | solution.py:60
  355.9 17.6 %multiply_convert_fusion = bf16[12,512,1024]{2,1,0:T(8,128)(2,1)S(1)} fusion(f32[12,512,1024]{2,1,0:T(8,128)} %get-tuple-element.71, f32[12,512,1024]{2,1,0:T(8,128)} %get-tuple-element.60, f32[12,512]{1,0:T(8,128)S(1)} %get-tuple-element.70, f32[12,512]{1,0:T(8,128)S(1)} %copy-done.38, pred[512,1024]{1,0:T(8,128)(4,1)} %get-tuple-element.56), kind=kLoop, calls=%fused_computation | loop fusion | flops 37748736 | bytes 63488000 | tf_op jit(solution)/shard_map/convert_element_type | solution.py:62
  423.9 9.9 %convolution_convert_fusion = bf16[3072,768]{1,0:T(8,128)(2,1)} fusion(bf16[1024,3072]{1,0:T(8,128)(2,1)} %get-tuple-element.65, f32[1024,768]{1,0:T(8,128)S(1)} %copy-done.28), kind=kOutput, calls=%fused_computation.28 | convolution fusion | flops 4834983936 | bytes 14155776 | tf_op jit(solution)/shard_map/dot_general | solution.py:24
  467.4 37.9 %collective-permute-done.1 = bf16[2,512,768]{2,1,0:T(8,128)(2,1)S(1)} collective-permute-done((bf16[2,512,768]{2,1,0:T(8,128)(2,1)S(1)}, bf16[2,512,768]{2,1,0:T(8,128)(2,1)S(1)}, u32[]{:S(2)}, u32[]{:S(2)}) %collective-permute-start.1) | collective-permute-done | bytes 1572896 | tf_op jit(solution)/shard_map/ppermute | solution.py:227
  507.7 13.3 %reduce-scatter.10.cloned.1.call-done = bf16[24,2432]{1,0:T(8,128)(2,1)} async-done(((bf16[768,2432]{1,0:T(8,128)(2,1)}), bf16[24,2432]{1,0:T(8,128)(2,1)}) %reduce-scatter.10.cloned.1.call-update) | async-done | bytes 116752
  525.6 107.6 %reduce-scatter.8.cloned.1.call-done = bf16[96,768]{1,0:T(8,128)(2,1)} async-done(((bf16[3072,768]{1,0:T(8,128)(2,1)}), bf16[96,768]{1,0:T(8,128)(2,1)}) %reduce-scatter.8.cloned.1.call-update) | async-done | bytes 147472 | tf_op jit(solution)/shard_map/reduce_scatter | solution.py:173
  634.8 116.1 %reduce-scatter.6.cloned.1.call-done = bf16[24,3840]{1,0:T(8,128)(2,1)} async-done(((bf16[768,3840]{1,0:T(8,128)(2,1)}), bf16[24,3840]{1,0:T(8,128)(2,1)}) %reduce-scatter.6.cloned.1.call-update) | async-done | bytes 184336 | tf_op jit(solution)/shard_map/reduce_scatter | solution.py:185
  (240 shorter events, 177.4 us)
Async XLA Ops:
  7.2 18.1 %copy-start.56 = (s32[1,2]{1,0:T(1,128)S(1)}, s32[1,2]{1,0:T(1,128)}, u32[]{:S(2)}) copy-start(s32[1,2]{1,0:T(1,128)} %param.34) | copy-start | bytes 28
  7.2 20.0 %copy-start = (bf16[1,2,512,768]{3,2,1,0:T(8,128)(2,1)S(1)}, bf16[1,2,512,768]{3,2,1,0:T(8,128)(2,1)}, u32[]{:S(2)}) copy-start(bf16[1,2,512,768]{3,2,1,0:T(8,128)(2,1)} %param.35) | copy-start | bytes 4718596
  7.2 72.9 %all-gather.4.cloned.1.call-start = ((), (), s32[]{:S(2)}) async-start(), calls=%async_computation.3 | async-start | bytes 3852288 | tf_op jit(solution)/shard_map/all_gather | solution.py:127
  15.7 163.9 %all-gather.6.cloned.1.call-start = ((), (), s32[]{:S(2)}) async-start(), calls=%async_computation.4 | async-start | bytes 6082560 | tf_op jit(solution)/shard_map/all_gather | solution.py:133
  17.4 197.8 %all-gather.8.cloned.1.call-start = ((), (), s32[]{:S(2)}) async-start(), calls=%async_computation.5 | async-start | bytes 4866048 | tf_op jit(solution)/shard_map/all_gather | solution.py:136
  19.1 44.5 %copy-start.21 = (bf16[1,2,512,768]{2,3,1,0:T(8,128)(2,1)}, bf16[1,2,512,768]{2,3,1,0:T(8,128)(2,1)S(1)}, u32[]{:S(2)}) copy-start(bf16[1,2,512,768]{2,3,1,0:T(8,128)(2,1)S(1)} %copy.104) | copy-start | bytes 4718596
  19.2 41.0 %collective-permute-start = (bf16[2,512,768]{1,2,0:T(8,128)(2,1)S(1)}, bf16[2,512,768]{1,2,0:T(8,128)(2,1)}, u32[]{:S(2)}, u32[]{:S(2)}) collective-permute-start(bf16[2,512,768]{1,2,0:T(8,128)(2,1)S(1)} %bitcast.126), channel_id=1, source_target_pairs={{0,16},{1,17},{2,18},{3,19},{4,20},{5,21},{6,22},{7,23},{8,24},{9,... | collective-permute-start | bytes 4718600 | tf_op jit(solution)/shard_map/ppermute | solution.py:104
  25.2 495.7 %reduce-scatter.10.cloned.1.call-start = ((), (), s32[]{:S(2)}) async-start(), calls=%async_computation.8 | async-start | bytes 3852288
  68.5 15.1 %copy-start.31 = (bf16[1,2,512,768]{3,2,1,0:T(8,128)(2,1)S(1)}, bf16[1,2,512,768]{3,2,1,0:T(8,128)(2,1)}, u32[]{:S(2)}) copy-start(bf16[1,2,512,768]{3,2,1,0:T(8,128)(2,1)} %param.18) | copy-start | bytes 4718596
  97.6 12.8 %copy-start.1 = (bf16[1,1024,768]{1,2,0:T(8,128)(2,1)}, bf16[1,1024,768]{1,2,0:T(8,128)(2,1)S(1)}, u32[]{:S(2)}) copy-start(bf16[1,1024,768]{1,2,0:T(8,128)(2,1)S(1)} %copy.117) | copy-start | bytes 4718596
  97.6 12.8 %copy-start.3 = (pred[512,1024]{1,0:T(8,128)(4,1)S(1)}, pred[512,1024]{1,0:T(8,128)(4,1)}, u32[]{:S(2)}) copy-start(pred[512,1024]{1,0:T(8,128)(4,1)} %get-tuple-element.56) | copy-start | bytes 1572868
  110.4 12.5 %copy-start.41 = (f32[12,512]{1,0:T(8,128)}, f32[12,512]{1,0:T(8,128)S(1)}, u32[]{:S(2)}) copy-start(f32[12,512]{1,0:T(8,128)S(1)} %get-tuple-element.59) | copy-start | bytes 73732
  130.7 24.6 %copy-start.37 = (f32[12,512]{1,0:T(8,128)}, f32[12,512]{1,0:T(8,128)S(1)}, u32[]{:S(2)}) copy-start(f32[12,512]{1,0:T(8,128)S(1)} %log_add_fusion) | copy-start | bytes 73732
  185.4 29.8 %copy-start.52 = (f32[768]{0:T(1024)S(1)}, f32[768]{0:T(1024)}, u32[]{:S(2)}) copy-start(f32[768]{0:T(1024)} %get-tuple-element.25) | copy-start | bytes 9220
  228.5 16.7 %slice-start.2 = ((s8[5898240]{0:T(1024)(128)(4,1)}), s8[4194304]{0:T(1024)(128)(4,1)S(1)}, s32[]{:S(2)}) async-start(s8[5898240]{0:T(1024)(128)(4,1)} %bitcast.156), calls=%async_computation.11 | async-start | bytes 8388608
  230.3 14.9 %copy-start.27 = (f32[1024,768]{1,0:T(8,128)}, f32[1024,768]{1,0:T(8,128)S(1)}, u32[]{:S(2)}) copy-start(f32[1024,768]{1,0:T(8,128)S(1)} %get-tuple-element.40) | copy-start | bytes 9437188
  230.3 14.9 %copy-start.10 = (f32[1024,768]{1,0:T(8,128)S(1)}, f32[1024,768]{1,0:T(8,128)}, u32[]{:S(2)}) copy-start(f32[1024,768]{1,0:T(8,128)} %copy-done.9) | copy-start | bytes 9437188
  230.3 14.9 %slice-start.3 = ((s8[5898240]{0:T(1024)(128)(4,1)}), s8[1703936]{0:T(1024)(128)(4,1)S(1)}, s32[]{:S(2)}) async-start(s8[5898240]{0:T(1024)(128)(4,1)} %bitcast.156), calls=%async_computation.12 | async-start | bytes 3407872
  321.7 12.9 %copy-start.6 = (pred[512,1024]{1,0:T(8,128)(4,1)S(1)}, pred[512,1024]{1,0:T(8,128)(4,1)}, u32[]{:S(2)}) copy-start(pred[512,1024]{1,0:T(8,128)(4,1)} %get-tuple-element.56) | copy-start | bytes 1572868
  321.8 12.9 %copy-start.15 = (bf16[1,1024,768]{1,2,0:T(8,128)(2,1)S(1)}, bf16[1,1024,768]{1,2,0:T(8,128)(2,1)}, u32[]{:S(2)}) copy-start(bf16[1,1024,768]{1,2,0:T(8,128)(2,1)} %copy.116) | copy-start | bytes 4718596
  321.8 12.9 %copy-start.30 = (bf16[512,768]{0,1:T(8,128)(2,1)S(1)}, bf16[512,768]{0,1:T(8,128)(2,1)}, u32[]{:S(2)}) copy-start(bf16[512,768]{0,1:T(8,128)(2,1)} %get-tuple-element.49) | copy-start | bytes 2359300
  422.1 211.1 %reduce-scatter.8.cloned.1.call-start = ((), (), s32[]{:S(2)}) async-start(), calls=%async_computation.7 | async-start | bytes 4866048 | tf_op jit(solution)/shard_map/reduce_scatter | solution.py:173
  433.9 316.9 %reduce-scatter.6.cloned.1.call-start = ((), (), s32[]{:S(2)}) async-start(), calls=%async_computation.6 | async-start | bytes 6082560 | tf_op jit(solution)/shard_map/reduce_scatter | solution.py:185
  463.3 41.9 %collective-permute-start.1 = (bf16[2,512,768]{2,1,0:T(8,128)(2,1)S(1)}, bf16[2,512,768]{2,1,0:T(8,128)(2,1)S(1)}, u32[]{:S(2)}, u32[]{:S(2)}) collective-permute-start(bf16[2,512,768]{2,1,0:T(8,128)(2,1)S(1)} %slice.274), channel_id=1, source_target_pairs={{16,0},{17,1},{18,2},{19,3},{20,4},{21,5},{22,6},{23,7},{24,8},{25... | collective-permute-start | bytes 4718600 | tf_op jit(solution)/shard_map/ppermute | solution.py:227
  (47 other events, 277.0 us)
Sparse Core Ops, SparseCore 0:
  15.8 64.2 all-gather.3
  83.6 66.3 all-gather.5
  152.8 62.2 all-gather.7
  422.2 98.7 reduce-scatter.9
  526.3 106.8 reduce-scatter.7
  638.6 112.1 reduce-scatter.5
where the time goes:
time: 765 us; the launch traced here: 761 us
  waiting for transfers between devices  336 us (44%)
  matrix products  242 us (32%)
  other arithmetic  90.9 us (12%)
  local copies, waits for them, and re-layouts  68 us (9%)
  between operations  16.4 us (2%)
    reduce_scatter x1, waiting for transfers between devices, on_device(): lax.psum_scatter(jnp.concatenate([g_output, g_inner], axis=1).astype(BF16...  116 us
    reduce_scatter x1, waiting for transfers between devices, on_device(): lax.psum_scatter(g_outer, BOTH, scatter_dimension=0, tiled=True).astype(F32)  108 us
    dot_general x2, matrix products, attend_back(): jnp.einsum('qhd,khd->hqk', grad_h, heads_of(v), preferred_element_type=F32)  43.2 us
    ppermute x1, waiting for transfers between devices, on_device(): lax.ppermute(via_kv[:, rows:].astype(BF16), 'seq', [(1, 0)]).astype(F32)  37.9 us
    dot_general x5, matrix products, dot_t(): lax.dot_general(a, b, (((1,), (1,)), ((), ())), preferred_element_type=F32)  35.8 us
    dot_general x5, matrix products, t_dot(): lax.dot_general(a, b, (((0,), (0,)), ((), ())), preferred_element_type=F32)  35.6 us
    convert_element_type x2, other arithmetic, attend_back(): grad_scores = (probs * (grad_probs - row_dot)).astype(BF16)  35.1 us
    dot_general x5, matrix products, dot(): return jnp.dot(a, b, preferred_element_type=F32)  30.3 us
  transfers between devices with their start and end apart: 8, of which 7 were waited for; matrix products, arithmetic and copies ran while one was open for 23% of the time, Pallas kernels for 0%

commit v1 on v0

--- a/solution.py
+++ b/solution.py
@@ -10,6 +10,16 @@
 BOTH = ("seq", "dp")
 F32 = jnp.float32
 BF16 = jnp.bfloat16
+
+
+def place_points(shard_in, shard_axis, array_dim):
+    return lax.all_to_all(
+        jnp.concatenate(lax.axis_size(shard_axis) * [shard_in], axis=array_dim),
+        axis_name=shard_axis,
+        split_axis=array_dim,
+        concat_axis=array_dim,
+        tiled=True,
+    )
 
 
 def dot(a, b):
@@ -133,7 +143,7 @@
     second_pack = lax.all_gather(
         jnp.concatenate([output_weight, inner_weight], axis=1), BOTH, axis=0, tiled=True
     )
-    full_outer = lax.all_gather(outer_weight, BOTH, axis=0, tiled=True)
+    full_outer = place_points(outer_weight, shard_axis=BOTH, array_dim=0)
     full_query = first_pack[:, :width]
     full_kv = first_pack[:, width : 3 * width]
     small_all = first_pack[:, 3 * width : 3 * width + small_count].astype(F32)

time: 765 us -> 789 us (1.031)
  waiting for transfers between devices: 336 us -> 350 us
    all_gather x1 -> x0, waiting for transfers between devices: 19.7 us -> none  [on_device(): full_outer = lax.all_gather(outer_weight, BOTH, axis=0, tiled=True)]
    ppermute x1, waiting for transfers between devices: 30.2 us -> 49.9 us  [on_device(): before = lax.ppermute(x, 'seq', [(0, 1)])]
    unnamed x7 -> x6, waiting for transfers between devices: 13.4 us -> 18.5 us
  transfers between devices with their start and end apart: 8 -> 8, of which waited for: 7 -> 6; matrix products, arithmetic and copies ran while one was open for 23% -> 23% of each run, Pallas kernels for 0% -> 0%
where the time goes in v1:
time: 789 us; the launch traced here: 785 us
  waiting for transfers between devices  350 us (44%)
  matrix products  244 us (31%)
  other arithmetic  90 us (11%)
  local copies, waits for them, and re-layouts  71.3 us (9%)
  between operations  16.3 us (2%)
  starting transfers between devices  12.6 us (2%)
    reduce_scatter x1, waiting for transfers between devices, on_device(): lax.psum_scatter(jnp.concatenate([g_output, g_inner], axis=1).astype(BF16...  116 us
    reduce_scatter x1, waiting for transfers between devices, on_device(): lax.psum_scatter(g_outer, BOTH, scatter_dimension=0, tiled=True).astype(F32)  107 us
    ppermute x1, waiting for transfers between devices, on_device(): before = lax.ppermute(x, 'seq', [(0, 1)])  49.9 us
    dot_general x2, matrix products, attend_back(): jnp.einsum('qhd,khd->hqk', grad_h, heads_of(v), preferred_element_type=F32)  43.2 us
    ppermute x1, waiting for transfers between devices, on_device(): lax.ppermute(via_kv[:, rows:].astype(BF16), 'seq', [(1, 0)]).astype(F32)  40.9 us
    dot_general x5, matrix products, dot_t(): lax.dot_general(a, b, (((1,), (1,)), ((), ())), preferred_element_type=F32)  36.2 us
    dot_general x5, matrix products, t_dot(): lax.dot_general(a, b, (((0,), (0,)), ((), ())), preferred_element_type=F32)  36.1 us
    convert_element_type x2, other arithmetic, attend_back(): grad_scores = (probs * (grad_probs - row_dot)).astype(BF16)  35.1 us
  transfers between devices with their start and end apart: 8, of which 6 were waited for; matrix products, arithmetic and copies ran while one was open for 23% of the time, Pallas kernels for 0%

profile of v1, /device:TPU:0, one launch (start us, length us, event | category | flops | bytes accessed | tf_op | source)
XLA Modules:
  0.0 784.9 jit_solution(10241211123313909443)
XLA Ops:
  40.4 49.9 %collective-permute-done = bf16[2,512,768]{1,2,0:T(8,128)(2,1)} collective-permute-done((bf16[2,512,768]{1,2,0:T(8,128)(2,1)S(1)}, bf16[2,512,768]{1,2,0:T(8,128)(2,1)}, u32[]{:S(2)}, u32[]{:S(2)}) %collective-permute-start) | collective-permute-done | bytes 1572896 | tf_op jit(solution)/shard_map/ppermute | solution.py:114
  98.6 17.9 %all-gather.3.cloned.1.call-done = bf16[768,2432]{1,0:T(8,128)(2,1)} async-done(((bf16[24,2432]{1,0:T(8,128)(2,1)}), bf16[768,2432]{1,0:T(8,128)(2,1)}) %all-gather.3.cloned.1.call-update) | async-done | bytes 3735568 | tf_op jit(solution)/shard_map/all_gather | solution.py:137
  136.4 10.6 %fusion.1 = (f32[12,512]{1,0:T(8,128)S(1)}, f32[12,512,1024]{2,1,0:T(8,128)}) fusion(pred[512,1024]{1,0:T(8,128)(4,1)S(1)} %copy-done.4, bf16[512,12,64]{0,2,1:T(8,128)(2,1)S(1)} %bitcast.117, bf16[1024,12,64]{0,2,1:T(8,128)(2,1)S(1)} %bitcast.113), kind=kOutput, calls=%fused_computation.11 | convolution fusion | flops 824174592 | bytes 28073984 | tf_op jit(solution)/shard_map/qhd,khd->hqk/dot_general | solution.py:56
  147.0 12.4 %exponential_reduce_fusion = f32[12,512]{1,0:T(8,128)} fusion(f32[12,512,1024]{2,1,0:T(8,128)} %get-tuple-element.60, f32[12,512]{1,0:T(8,128)S(1)} %get-tuple-element.59, pred[512,1024]{1,0:T(8,128)(4,1)S(1)} %copy-done.4), kind=kLoop, calls=%fused_computation.5 | loop fusion | flops 25159680 | bytes 25739264 | tf_op jit(solution)/shard_map/reduce_sum | solution.py:60
  167.4 12.7 %fusion = (f32[12,512]{1,0:T(8,128)S(1)}, f32[12,512,1024]{2,1,0:T(8,128)}) fusion(pred[512,1024]{1,0:T(8,128)(4,1)} %get-tuple-element.55, bf16[512,12,64]{0,2,1:T(8,128)(2,1)} %bitcast.119, bf16[1024,12,64]{0,2,1:T(8,128)(2,1)S(1)} %bitcast.115), kind=kOutput, calls=%fused_computation.10 | convolution fusion | flops 824174592 | bytes 28073984 | tf_op jit(solution)/shard_map/qhd,khd->hqk/dot_general | solution.py:56
  180.1 12.2 %exponential_reduce_fusion.1 = f32[12,512]{1,0:T(8,128)S(1)} fusion(f32[12,512,1024]{2,1,0:T(8,128)} %get-tuple-element.62, f32[12,512]{1,0:T(8,128)S(1)} %get-tuple-element.61, pred[512,1024]{1,0:T(8,128)(4,1)S(1)} %copy-done.8), kind=kLoop, calls=%fused_computation.8 | loop fusion | flops 25159680 | bytes 25739264 | tf_op jit(solution)/shard_map/reduce_sum | solution.py:60
  192.4 12.1 %convolution_convert_fusion.7 = bf16[12,64,512]{2,1,0:T(8,128)(2,1)} fusion(bf16[1024,12,64]{0,2,1:T(8,128)(2,1)S(1)} %bitcast.123, f32[12,512,1024]{2,1,0:T(8,128)} %get-tuple-element.60, f32[12,512]{1,0:T(8,128)S(1)} %log_add_fusion, pred[512,1024]{1,0:T(8,128)(4,1)S(1)} %copy-done.5), kind=kOutput, calls=%fused_computation.85 | convolution fusion | flops 830865408 | bytes 28073984 | tf_op jit(solution)/shard_map/hqk,khd->qhd/dot_general | solution.py:63
  204.4 11.9 %convolution_convert_fusion.8 = bf16[12,64,512]{2,1,0:T(8,128)(2,1)} fusion(bf16[1024,12,64]{0,2,1:T(8,128)(2,1)S(1)} %bitcast.125, f32[12,512,1024]{2,1,0:T(8,128)} %get-tuple-element.62, f32[12,512]{1,0:T(8,128)S(1)} %log_add_fusion.1, pred[512,1024]{1,0:T(8,128)(4,1)S(1)} %copy-done.8), kind=kOutput, calls=%fused_computation.86 | convolution fusion | flops 830865408 | bytes 28073984 | tf_op jit(solution)/shard_map/hqk,khd->qhd/dot_general | solution.py:63
  222.1 10.1 %multiply_convert_fusion.2 = (bf16[1024,3072]{1,0:T(8,128)(2,1)}, f32[1024,3072]{1,0:T(8,128)}) fusion(f32[3072]{0:T(1024)S(1)} %add.172, bf16[768,3840]{1,0:T(8,128)(2,1)S(1)} %copy-done.57, f32[1024,768]{1,0:T(8,128)S(1)} %get-tuple-element.64, f32[768]{0:T(1024)S(1)} %copy-done.51, f32[768]{0:T(1024)S(1)} %get-tuple-element.27, ...), kind=kOutput, calls=%fused_computation.21 | convolution fusion | flops 4854644736 | bytes 26767360 | tf_op jit(solution)/shard_map/dot_general | solution.py:26
  232.2 9.3 %fusion.72 = (f32[1024]{0:T(1024)S(1)}, f32[1024,768]{1,0:T(8,128)S(1)}) fusion(f32[768]{0:T(1024)S(1)} %copy-done.53, bf16[1024,3072]{1,0:T(8,128)(2,1)} %get-tuple-element.65, bf16[3072,768]{1,0:T(8,128)(2,1)} %bitcast.26, f32[768]{0:T(1024)S(1)} %copy-done.51, f32[768]{0:T(1024)S(1)} %get-tuple-element.27, f32[1024]{0:T(1024)S(1)} %add_rsqrt_fusion.1, ...), kind=kOutput, calls=%fused_computation.187 | convolution fusion | flops 4837342208 | bytes 17323008 | tf_op jit(solution)/shard_map/dot_general | solution.py:26
  247.2 15.4 %fusion.73 = (bf16[3072]{0:T(1024)(128)(2,1)}, bf16[1024,3072]{1,0:T(8,128)(2,1)}) fusion(f32[1024,3072]{1,0:T(8,128)} %get-tuple-element.66, f32[3072]{0:T(1024)S(1)} %add.172, bf16[3072,768]{1,0:T(8,128)(2,1)} %bitcast.26, f32[1024,768]{1,0:T(8,128)S(1)} %get-tuple-element.40), kind=kOutput, calls=%fused_computation.188 | convolution fusion | flops 4876661760 | bytes 26757120 | tf_op jit(solution)/shard_map/dot_general | solution.py:30
  262.6 8.8 %multiply_reduce_fusion.2 = (bf16[768]{0:T(1024)(128)(2,1)}, f32[1024]{0:T(1024)S(1)}, f32[1024]{0:T(1024)S(1)}, bf16[768]{0:T(1024)(128)(2,1)}, f32[1024,768]{1,0:T(8,128)S(1)}) fusion(f32[1024,768]{1,0:T(8,128)S(1)} %copy-done.11, f32[1024]{0:T(1024)S(1)} %add_rsqrt_fusion.1, f32[1024]{0:T(1024)S(1)} %broadcast_multiply_fusion.4, ...), kind=kOutput, calls=%fused_computation.52 | convolution fusion | flops 4839698432 | bytes 20470784 | tf_op jit(solution)/shard_map/dot_general | solution.py:30
  275.6 12.7 %convolution_convert_fusion.3 = bf16[12,64,1024]{2,1,0:T(8,128)(2,1)} fusion(bf16[512,12,64]{0,2,1:T(8,128)(2,1)S(1)} %bitcast.136, f32[12,512,1024]{2,1,0:T(8,128)} %get-tuple-element.62, f32[12,512]{1,0:T(8,128)S(1)} %copy-done.40, pred[512,1024]{1,0:T(8,128)(4,1)S(1)} %copy-done.9), kind=kOutput, calls=%fused_computation.75 | convolution fusion | flops 831258624 | bytes 28073984 | tf_op jit(solution)/shard_map/hqk,qhd->khd/dot_general | solution.py:75
  288.3 21.9 %multiply_reduce_fusion.1 = (f32[12,512]{1,0:T(8,128)}, f32[12,512,1024]{2,1,0:T(8,128)}) fusion(f32[12,512,1024]{2,1,0:T(8,128)} %get-tuple-element.62, f32[12,512]{1,0:T(8,128)S(1)} %copy-done.40, pred[512,1024]{1,0:T(8,128)(4,1)S(1)} %copy-done.9, bf16[512,12,64]{0,2,1:T(8,128)(2,1)S(1)} %bitcast.137, bf16[1024,12,64]{0,2,1:T(8,128)(2,1)S(1)} %bitcast.126), kind=kOutput, calls=%fused_computation.3 | convolution fusion | flops 836757504 | bytes 53264384 | tf_op jit(solution)/shard_map/qhd,khd->hqk/dot_general | solution.py:70
  310.2 17.5 %multiply_convert_fusion.1 = bf16[12,512,1024]{2,1,0:T(8,128)(2,1)S(1)} fusion(f32[12,512,1024]{2,1,0:T(8,128)} %get-tuple-element.73, f32[12,512,1024]{2,1,0:T(8,128)} %get-tuple-element.62, f32[12,512]{1,0:T(8,128)} %get-tuple-element.72, f32[12,512]{1,0:T(8,128)} %copy-done.39, pred[512,1024]{1,0:T(8,128)(4,1)} %get-tuple-element.55), kind=kLoop, calls=%fused_computation.2 | loop fusion | flops 37748736 | bytes 63488000 | tf_op jit(solution)/shard_map/convert_element_type | solution.py:72
  338.7 12.8 %convolution_convert_fusion.2 = bf16[12,64,1024]{2,1,0:T(8,128)(2,1)} fusion(bf16[512,12,64]{0,2,1:T(8,128)(2,1)S(1)} %bitcast.134, f32[12,512,1024]{2,1,0:T(8,128)} %get-tuple-element.60, f32[12,512]{1,0:T(8,128)S(1)} %copy-done.38, pred[512,1024]{1,0:T(8,128)(4,1)S(1)} %copy-done.6), kind=kOutput, calls=%fused_computation.74 | convolution fusion | flops 831258624 | bytes 28073984 | tf_op jit(solution)/shard_map/hqk,qhd->khd/dot_general | solution.py:75
  351.6 21.3 %multiply_reduce_fusion = (f32[12,512]{1,0:T(8,128)S(1)}, f32[12,512,1024]{2,1,0:T(8,128)}) fusion(f32[12,512,1024]{2,1,0:T(8,128)} %get-tuple-element.60, f32[12,512]{1,0:T(8,128)S(1)} %copy-done.38, pred[512,1024]{1,0:T(8,128)(4,1)S(1)} %copy-done.7, bf16[512,12,64]{0,2,1:T(8,128)(2,1)S(1)} %bitcast.135, bf16[1024,12,64]{0,2,1:T(8,128)(2,1)S(1)} %bitcast.124), kind=kOutput, calls=%fused_computation.1 | convolution fusion | flops 836757504 | bytes 53264384 | tf_op jit(solution)/shard_map/qhd,khd->hqk/dot_general | solution.py:70
  372.9 17.6 %multiply_convert_fusion = bf16[12,512,1024]{2,1,0:T(8,128)(2,1)S(1)} fusion(f32[12,512,1024]{2,1,0:T(8,128)} %get-tuple-element.71, f32[12,512,1024]{2,1,0:T(8,128)} %get-tuple-element.60, f32[12,512]{1,0:T(8,128)S(1)} %get-tuple-element.70, f32[12,512]{1,0:T(8,128)S(1)} %copy-done.38, pred[512,1024]{1,0:T(8,128)(4,1)} %get-tuple-element.56), kind=kLoop, calls=%fused_computation | loop fusion | flops 37748736 | bytes 63488000 | tf_op jit(solution)/shard_map/convert_element_type | solution.py:72
  440.5 9.8 %convolution_convert_fusion = bf16[3072,768]{1,0:T(8,128)(2,1)} fusion(bf16[1024,3072]{1,0:T(8,128)(2,1)} %get-tuple-element.65, f32[1024,768]{1,0:T(8,128)S(1)} %copy-done.30), kind=kOutput, calls=%fused_computation.28 | convolution fusion | flops 4834983936 | bytes 14155776 | tf_op jit(solution)/shard_map/dot_general | solution.py:34
  458.1 8.7 %convolution_convert_fusion.1 = bf16[768,3072]{1,0:T(8,128)(2,1)S(1)} fusion(bf16[1024,3072]{1,0:T(8,128)(2,1)} %get-tuple-element.79, f32[1024,768]{1,0:T(8,128)S(1)} %copy-done.12, f32[768]{0:T(1024)S(1)} %copy-done.52, f32[768]{0:T(1024)S(1)} %get-tuple-element.27, f32[1024]{0:T(1024)S(1)} %add_rsqrt_fusion.1, f32[1024]{0:T(1024)S(1)} %broadcast_multiply_fusion.4), kind=kOutput, calls=%fused_computation.29 | convolution fusion | flops 4838129664 | bytes 14170112 | tf_op jit(solution)/shard_map/dot_general | solution.py:34
  483.9 40.9 %collective-permute-done.1 = bf16[2,512,768]{2,1,0:T(8,128)(2,1)S(1)} collective-permute-done((bf16[2,512,768]{2,1,0:T(8,128)(2,1)S(1)}, bf16[2,512,768]{2,1,0:T(8,128)(2,1)S(1)}, u32[]{:S(2)}, u32[]{:S(2)}) %collective-permute-start.1) | collective-permute-done | bytes 1572896 | tf_op jit(solution)/shard_map/ppermute | solution.py:237
  527.2 18.4 %reduce-scatter.10.cloned.1.call-done = bf16[24,2432]{1,0:T(8,128)(2,1)} async-done(((bf16[768,2432]{1,0:T(8,128)(2,1)}), bf16[24,2432]{1,0:T(8,128)(2,1)}) %reduce-scatter.10.cloned.1.call-update) | async-done | bytes 116752
  550.2 107.3 %reduce-scatter.8.cloned.1.call-done = bf16[96,768]{1,0:T(8,128)(2,1)} async-done(((bf16[3072,768]{1,0:T(8,128)(2,1)}), bf16[96,768]{1,0:T(8,128)(2,1)}) %reduce-scatter.8.cloned.1.call-update) | async-done | bytes 147472 | tf_op jit(solution)/shard_map/reduce_scatter | solution.py:183
  659.1 116.0 %reduce-scatter.6.cloned.1.call-done = bf16[24,3840]{1,0:T(8,128)(2,1)} async-done(((bf16[768,3840]{1,0:T(8,128)(2,1)}), bf16[24,3840]{1,0:T(8,128)(2,1)}) %reduce-scatter.6.cloned.1.call-update) | async-done | bytes 184336 | tf_op jit(solution)/shard_map/reduce_scatter | solution.py:195
  (263 shorter events, 180.4 us)
Async XLA Ops:
  7.2 19.9 %copy-start = (bf16[96,768]{1,0:T(8,128)(2,1)S(1)}, bf16[96,768]{1,0:T(8,128)(2,1)}, u32[]{:S(2)}) copy-start(bf16[96,768]{1,0:T(8,128)(2,1)} %param.30) | copy-start | bytes 442372
  7.2 109.3 %all-gather.3.cloned.1.call-start = ((), (), s32[]{:S(2)}) async-start(), calls=%async_computation.4 | async-start | bytes 3852288 | tf_op jit(solution)/shard_map/all_gather | solution.py:137
  17.3 73.0 %copy-start.23 = (bf16[1,2,512,768]{2,3,1,0:T(8,128)(2,1)}, bf16[1,2,512,768]{2,3,1,0:T(8,128)(2,1)S(1)}, u32[]{:S(2)}) copy-start(bf16[1,2,512,768]{2,3,1,0:T(8,128)(2,1)S(1)} %copy.104) | copy-start | bytes 4718596
  17.3 72.9 %collective-permute-start = (bf16[2,512,768]{1,2,0:T(8,128)(2,1)S(1)}, bf16[2,512,768]{1,2,0:T(8,128)(2,1)}, u32[]{:S(2)}, u32[]{:S(2)}) collective-permute-start(bf16[2,512,768]{1,2,0:T(8,128)(2,1)S(1)} %bitcast.128), channel_id=1, source_target_pairs={{0,16},{1,17},{2,18},{3,19},{4,20},{5,21},{6,22},{7,23},{8,24},{9,... | collective-permute-start | bytes 4718600 | tf_op jit(solution)/shard_map/ppermute | solution.py:114
  29.8 202.3 %all-to-all-start = ((bf16[32,96,768]{2,1,0:T(8,128)(2,1)}), bf16[32,96,768]{2,1,0:T(8,128)(2,1)}, u32[]{:S(2)}, u32[]{:S(2)}) async-start(bf16[32,96,768]{2,1,0:T(8,128)(2,1)} %bitcast.131), calls=%async_computation | async-start | bytes 9437184 | tf_op jit(solution)/shard_map/all_to_all | solution.py:16
  34.9 181.5 %all-gather.5.cloned.1.call-start = ((), (), s32[]{:S(2)}) async-start(), calls=%async_computation.5 | async-start | bytes 6082560 | tf_op jit(solution)/shard_map/all_gather | solution.py:143
  35.6 509.9 %reduce-scatter.10.cloned.1.call-start = ((), (), s32[]{:S(2)}) async-start(), calls=%async_computation.8 | async-start | bytes 3852288
  147.0 12.4 %copy-start.41 = (f32[12,512]{1,0:T(8,128)}, f32[12,512]{1,0:T(8,128)S(1)}, u32[]{:S(2)}) copy-start(f32[12,512]{1,0:T(8,128)S(1)} %get-tuple-element.59) | copy-start | bytes 73732
  161.6 18.5 %copy-start.3 = (bf16[1,1024,768]{1,2,0:T(8,128)(2,1)}, bf16[1,1024,768]{1,2,0:T(8,128)(2,1)S(1)}, u32[]{:S(2)}) copy-start(bf16[1,1024,768]{1,2,0:T(8,128)(2,1)S(1)} %copy.115) | copy-start | bytes 4718596
  167.3 25.0 %copy-start.37 = (f32[12,512]{1,0:T(8,128)}, f32[12,512]{1,0:T(8,128)S(1)}, u32[]{:S(2)}) copy-start(f32[12,512]{1,0:T(8,128)S(1)} %log_add_fusion) | copy-start | bytes 73732
  167.4 12.7 %copy-start.8 = (pred[512,1024]{1,0:T(8,128)(4,1)S(1)}, pred[512,1024]{1,0:T(8,128)(4,1)}, u32[]{:S(2)}) copy-start(pred[512,1024]{1,0:T(8,128)(4,1)} %get-tuple-element.55) | copy-start | bytes 1572868
  180.1 12.3 %copy-start.5 = (pred[512,1024]{1,0:T(8,128)(4,1)S(1)}, pred[512,1024]{1,0:T(8,128)(4,1)}, u32[]{:S(2)}) copy-start(pred[512,1024]{1,0:T(8,128)(4,1)} %get-tuple-element.56) | copy-start | bytes 1572868
  180.1 12.3 %copy-start.16 = (bf16[1,1024,768]{1,2,0:T(8,128)(2,1)S(1)}, bf16[1,1024,768]{1,2,0:T(8,128)(2,1)}, u32[]{:S(2)}) copy-start(bf16[1,1024,768]{1,2,0:T(8,128)(2,1)} %copy.116) | copy-start | bytes 4718596
  192.3 12.1 %copy-start.39 = (f32[12,512]{1,0:T(8,128)}, f32[12,512]{1,0:T(8,128)S(1)}, u32[]{:S(2)}) copy-start(f32[12,512]{1,0:T(8,128)S(1)} %log_add_fusion.1) | copy-start | bytes 73732
  245.4 17.1 %slice-start = ((s8[5898240]{0:T(1024)(128)(4,1)}), s8[4194304]{0:T(1024)(128)(4,1)S(1)}, s32[]{:S(2)}) async-start(s8[5898240]{0:T(1024)(128)(4,1)} %bitcast.157), calls=%async_computation.9 | async-start | bytes 8388608
  247.2 15.4 %copy-start.29 = (f32[1024,768]{1,0:T(8,128)}, f32[1024,768]{1,0:T(8,128)S(1)}, u32[]{:S(2)}) copy-start(f32[1024,768]{1,0:T(8,128)S(1)} %get-tuple-element.40) | copy-start | bytes 9437188
  247.2 15.4 %copy-start.11 = (f32[1024,768]{1,0:T(8,128)S(1)}, f32[1024,768]{1,0:T(8,128)}, u32[]{:S(2)}) copy-start(f32[1024,768]{1,0:T(8,128)} %copy-done.10) | copy-start | bytes 9437188
  247.2 15.4 %slice-start.1 = ((s8[5898240]{0:T(1024)(128)(4,1)}), s8[1703936]{0:T(1024)(128)(4,1)S(1)}, s32[]{:S(2)}) async-start(s8[5898240]{0:T(1024)(128)(4,1)} %bitcast.157), calls=%async_computation.10 | async-start | bytes 3407872
  338.7 12.9 %copy-start.7 = (pred[512,1024]{1,0:T(8,128)(4,1)S(1)}, pred[512,1024]{1,0:T(8,128)(4,1)}, u32[]{:S(2)}) copy-start(pred[512,1024]{1,0:T(8,128)(4,1)} %get-tuple-element.56) | copy-start | bytes 1572868
  338.7 12.9 %copy-start.17 = (bf16[1,1024,768]{1,2,0:T(8,128)(2,1)S(1)}, bf16[1,1024,768]{1,2,0:T(8,128)(2,1)}, u32[]{:S(2)}) copy-start(bf16[1,1024,768]{1,2,0:T(8,128)(2,1)} %copy.116) | copy-start | bytes 4718596
  338.7 12.9 %copy-start.32 = (bf16[512,768]{0,1:T(8,128)(2,1)S(1)}, bf16[512,768]{0,1:T(8,128)(2,1)}, u32[]{:S(2)}) copy-start(bf16[512,768]{0,1:T(8,128)(2,1)} %get-tuple-element.49) | copy-start | bytes 2359300
  439.4 218.1 %reduce-scatter.8.cloned.1.call-start = ((), (), s32[]{:S(2)}) async-start(), calls=%async_computation.7 | async-start | bytes 4866048 | tf_op jit(solution)/shard_map/reduce_scatter | solution.py:183
  450.4 324.7 %reduce-scatter.6.cloned.1.call-start = ((), (), s32[]{:S(2)}) async-start(), calls=%async_computation.6 | async-start | bytes 6082560 | tf_op jit(solution)/shard_map/reduce_scatter | solution.py:195
  479.8 45.0 %collective-permute-start.1 = (bf16[2,512,768]{2,1,0:T(8,128)(2,1)S(1)}, bf16[2,512,768]{2,1,0:T(8,128)(2,1)S(1)}, u32[]{:S(2)}, u32[]{:S(2)}) collective-permute-start(bf16[2,512,768]{2,1,0:T(8,128)(2,1)S(1)} %slice.274), channel_id=1, source_target_pairs={{16,0},{17,1},{18,2},{19,3},{20,4},{21,5},{22,6},{23,7},{24,8},{25... | collective-permute-start | bytes 4718600 | tf_op jit(solution)/shard_map/ppermute | solution.py:237
  (44 other events, 277.9 us)
Sparse Core Ops, SparseCore 0:
  15.7 100.6 all-gather.2
  119.9 70.7 all-gather.4
  439.5 106.0 reduce-scatter.9
  550.9 106.5 reduce-scatter.7
  663.0 112.0 reduce-scatter.5
